TPU v7x, 32 devices: a whole 2x2x4 slice. The times are simulated.
32 devices in a mesh: train: 2 (over y), tp: 8 (over z, x), dp: 2 (over core).
Axes of the slice: x: 2, y: 2, z: 4, core: 2. Of those that a mesh axis runs over, the one named last changes fastest.
Arguments:
- adapter_down_factor: bfloat16 [2, 2, 64, 8192], P(None, None, None, ('train', 'tp')), may hold values from -6 to 6
- adapter_up_factor: bfloat16 [2, 2, 1024, 64], P(None, None, ('train', 'tp')), may hold values from -0.75 to 0.75
- projection_weight: bfloat16 [2, 2, 1024, 8192], P(None, None, 'tp'), may hold values from -6 to 6
Outputs:
- merged: bfloat16 [2, 2, 1024, 8192], P(None, None, 'tp')
All inputs are finite; a program needn't handle non-finite values.
Results may differ from a plain program's by a relative error of at most 0.001.
Values may be sent and summed in bfloat16 or wider, within the bound.
A program may use at most 64 MiB of HBM per device.

v0:
```python
import jax
import jax.numpy as jnp
from jax import lax
from jax.sharding import PartitionSpec as P

adapter_scale = 2.0


def per_device(adapter_down_factor, adapter_up_factor, projection_weight):
    per_rows = projection_weight.shape[2]
    all_up_factors = lax.all_gather(adapter_up_factor, ("train", "tp"), axis=2, tiled=True)
    offset = lax.axis_index("tp") * per_rows
    b_rows = lax.dynamic_slice_in_dim(all_up_factors, offset, per_rows, 2)
    weight_block = projection_weight.astype(jnp.float32)
    weight_update = jnp.einsum(
        "eitd,eidh->eith",
        b_rows,
        lax.all_gather(adapter_down_factor, ("train", "tp"), axis=3, tiled=True),
        preferred_element_type=jnp.float32,
    )
    return (weight_block + adapter_scale * weight_update).astype(jnp.bfloat16)


def solution(mesh):
    in_specs = (
        P(None, None, None, ("train", "tp")),
        P(None, None, ("train", "tp"), None),
        P(None, None, "tp", None),
    )
    out_specs = P(None, None, "tp", None)
    return jax.shard_map(
        per_device, mesh=mesh, in_specs=in_specs, out_specs=out_specs, check_vma=False
    )
```

profile of v0, /device:TPU:0, one launch (start us, length us, event | category | flops | bytes accessed | tf_op | source)
XLA Modules:
  0.0 113.6 jit_solution(2396535174543031142)
XLA Ops:
  6.5 0.0 all-gather.2.cloned.1.call-start
  6.5 0.7 all-gather.2.cloned.1.call-update
  7.3 0.9 copy.5
  8.2 51.4 %all_gather.6 = bf16[2,2,1024,64]{3,1,0,2:T(2,128)(2,1)S(1)} all-gather(bf16[2,2,64,64]{3,1,0,2:T(2,128)(2,1)S(1)} %copy.5), channel_id=1, replica_groups=mesh['train'=2,'tp'=8,'dp'=2] {'train','tp'}, dimensions={2}, use_global_device_ids=true | all-gather | bytes 557056 | tf_op jit(solution)/shard_map/all_gather | solution.py:11
  59.5 0.1 constant_dynamic-slice_fusion
  59.6 39.0 %all-gather.2.cloned.1.call-done = bf16[2,2,64,8192]{3,2,1,0:T(8,128)(2,1)} async-done(((bf16[2,2,64,512]{3,2,1,0:T(8,128)(2,1)}), bf16[2,2,64,8192]{3,2,1,0:T(8,128)(2,1)}) %all-gather.2.cloned.1.call-update) | async-done | bytes 4194320 | tf_op jit(solution)/shard_map/all_gather | solution.py:18
  98.6 8.2 %add_convert_fusion = bf16[2,2,128,8192]{3,2,1,0:T(8,128)(2,1)} fusion(bf16[2,2,128,8192]{3,2,1,0:T(8,128)(2,1)} %param.5, bf16[2,2,64,8192]{3,2,1,0:T(8,128)(2,1)} %all-gather.2.cloned.1.call-done, bf16[2,2,128,64]{3,1,0,2:T(2,128)(2,1)S(1)} %constant_dynamic-slice_fusion), kind=kOutput, calls=%fused_computation | convolution fusion | flops 553648128 | bytes 21037056 | tf_op jit(solution)/shard_map/eitd,eidh->eith/dot_general | solution.py:15
Async XLA Ops:
  6.5 92.0 %all-gather.2.cloned.1.call-start = ((), (), s32[]{:S(2)}) async-start(), calls=%async_computation | async-start | bytes 4456448 | tf_op jit(solution)/shard_map/all_gather | solution.py:18
Sparse Core Ops, SparseCore 0:
  10.1 88.4 all-gather.1
where the time goes:
time: 114 us
  blocking collectives  51.4 us (45%)
  waiting for transfers between devices  39.7 us (35%)
  between operations  13.4 us (12%)
  matrix products  8.17 us (7%)
    all_gather x1, blocking collectives, per_device(): lax.all_gather(adapter_up_factor, ('train', 'tp'), axis=2, tiled=True)  51.4 us
    all_gather x1, waiting for transfers between devices, per_device(): lax.all_gather(adapter_down_factor, ('train', 'tp'), axis=3, tiled=True)  39 us
    dot_general x1, matrix products, per_device(): jnp.einsum('eitd,eidh->eith', b_rows, lax.all_gather(adapter_down_factor,...  8.17 us
  transfers between devices with their start and end apart: 1, of which 1 were waited for; matrix products, arithmetic and copies ran while one was open for 1% of the time, Pallas kernels for 0%

commit v1 on v0

--- a/solution.py
+++ b/solution.py
@@ -15,7 +15,7 @@
     weight_update = jnp.einsum(
         "eitd,eidh->eith",
         b_rows,
-        lax.all_gather(adapter_down_factor, ("train", "tp"), axis=3, tiled=True),
+        jnp.concatenate(lax.all_gather(adapter_down_factor, ("train", "tp")), axis=3),
         preferred_element_type=jnp.float32,
     )
     return (weight_block + adapter_scale * weight_update).astype(jnp.bfloat16)

time: 114 us -> 123 us (1.079)
  local copies, waits for them, and re-layouts: 1 us -> 15 us
  waiting for transfers between devices: 39.7 us -> 33.1 us
  blocking collectives: 51.4 us -> 53.2 us
    reshape x0 -> x1, local copies, waits for them, and re-layouts: none -> 7.38 us  [per_device(): jnp.concatenate(lax.all_gather(adapter_down_factor, ('train', 'tp')), axi...]
    all_gather x1, waiting for transfers between devices: 39 us -> 32.4 us  [per_device(): lax.all_gather(adapter_down_factor, ('train', 'tp'))]
    all_gather x0 -> x1, local copies, waits for them, and re-layouts: none -> 6.59 us  [per_device(): lax.all_gather(adapter_down_factor, ('train', 'tp'))]
    all_gather x1, blocking collectives: 51.4 us -> 53.2 us  [per_device(): lax.all_gather(adapter_up_factor, ('train', 'tp'), axis=2, tiled=True)]
where the time goes in v1:
time: 123 us
  blocking collectives  53.2 us (43%)
  waiting for transfers between devices  33.1 us (27%)
  local copies, waits for them, and re-layouts  15 us (12%)
  between operations  13.4 us (11%)
  matrix products  8.17 us (7%)
    all_gather x1, blocking collectives, per_device(): lax.all_gather(adapter_up_factor, ('train', 'tp'), axis=2, tiled=True)  53.2 us
    all_gather x1, waiting for transfers between devices, per_device(): lax.all_gather(adapter_down_factor, ('train', 'tp'))  32.4 us
    dot_general x1, matrix products, per_device(): jnp.einsum('eitd,eidh->eith', b_rows, jnp.concatenate(lax.all_gather(adap...  8.17 us
    reshape x1, local copies, waits for them, and re-layouts, per_device(): jnp.concatenate(lax.all_gather(adapter_down_factor, ('train', 'tp')), axi...  7.38 us
    all_gather x1, local copies, waits for them, and re-layouts, per_device(): lax.all_gather(adapter_down_factor, ('train', 'tp'))  6.59 us
  transfers between devices with their start and end apart: 1, of which 1 were waited for; matrix products, arithmetic and copies ran while one was open for 1% of the time, Pallas kernels for 0%

profile of v1, /device:TPU:0, one launch (start us, length us, event | category | flops | bytes accessed | tf_op | source)
XLA Modules:
  0.0 122.8 jit_solution(570417160657447954)
XLA Ops:
  6.5 0.0 all-gather.3.cloned.1.call-start
  6.5 0.7 all-gather.3.cloned.1.call-update
  7.3 0.9 copy.6
  8.2 53.2 %all_gather.9 = bf16[2,2,1024,64]{3,1,0,2:T(2,128)(2,1)S(1)} all-gather(bf16[2,2,64,64]{3,1,0,2:T(2,128)(2,1)S(1)} %copy.6), channel_id=1, replica_groups=mesh['train'=2,'tp'=8,'dp'=2] {'train','tp'}, dimensions={2}, use_global_device_ids=true | all-gather | bytes 557056 | tf_op jit(solution)/shard_map/all_gather | solution.py:11
  61.4 0.1 constant_dynamic-slice_fusion
  61.5 32.4 %all-gather.3.cloned.1.call-done = bf16[32,2,64,512]{3,2,1,0:T(8,128)(2,1)} async-done(((bf16[2,2,64,512]{3,2,1,0:T(8,128)(2,1)}), bf16[32,2,64,512]{3,2,1,0:T(8,128)(2,1)}) %all-gather.3.cloned.1.call-update) | async-done | bytes 4194320 | tf_op jit(solution)/shard_map/all_gather | solution.py:18
  93.8 6.6 %copy.13 = bf16[16,2,2,64,512]{4,0,3,2,1:T(8,128)(2,1)} copy(bf16[16,2,2,64,512]{4,3,2,1,0:T(8,128)(2,1)} %bitcast.8) | data formatting | bytes 8388608 | tf_op jit(solution)/shard_map/all_gather | solution.py:18
  100.4 7.4 %reshape.7 = bf16[2,2,64,8192]{3,2,1,0:T(8,128)(2,1)} reshape(bf16[2,2,64,16,512]{4,3,2,1,0:T(8,128)(2,1)} %bitcast.7) | data formatting | bytes 8388608 | tf_op jit(solution)/shard_map/reshape | solution.py:18
  107.8 8.2 %add_convert_fusion = bf16[2,2,128,8192]{3,2,1,0:T(8,128)(2,1)} fusion(bf16[2,2,128,8192]{3,2,1,0:T(8,128)(2,1)} %param.5, bf16[2,2,64,8192]{3,2,1,0:T(8,128)(2,1)} %reshape.7, bf16[2,2,128,64]{3,1,0,2:T(2,128)(2,1)S(1)} %constant_dynamic-slice_fusion), kind=kOutput, calls=%fused_computation | convolution fusion | flops 553648128 | bytes 21037056 | tf_op jit(solution)/shard_map/eitd,eidh->eith/dot_general | solution.py:15
Async XLA Ops:
  6.5 87.3 %all-gather.3.cloned.1.call-start = ((), (), s32[]{:S(2)}) async-start(), calls=%async_computation | async-start | bytes 4456448 | tf_op jit(solution)/shard_map/all_gather | solution.py:18
Sparse Core Ops, SparseCore 0:
  10.1 83.6 all-gather.2
